TPU v7x, 32 devices: a whole 2x2x4 slice. The times are simulated.
32 devices in a mesh: rows: 8 (over z, y), groups: 4 (over x, core).
Axes of the slice: x: 2, y: 2, z: 4, core: 2. Of those that a mesh axis runs over, the one named last changes fastest.
Arguments:
- basis: bfloat16 [8, 131072, 128], P(None, ('rows', 'groups')), may hold values from -6 to 6
- image: bfloat16 [8, 131072, 128], P(None, ('rows', 'groups')), may hold values from -6 to 6
- selection: int32 [8, 64], replicated, may hold values from 0 to 127, all different within a row
Outputs:
- rotated: bfloat16 [8, 131072, 128], P(None, ('rows', 'groups'))
Inputs may be any that keep to these rules, and one draw needn't show every extreme that they name: Each row of selection names 64 different columns.
All inputs are finite; a program needn't handle non-finite values.
Results may differ from a plain program's by a relative error of at most 0.005.
Values may be sent and summed in bfloat16 or wider, within the bound.
A program may use at most 128 MiB of HBM per device.

v0:
```python
import jax
import jax.numpy as jnp
from jax import lax
from jax.sharding import PartitionSpec as P

ITERS = 3


def small_solve(grams, chosen, total_rows):
    gram_s, cross, gram_f = (grams[0], grams[1], grams[2])
    width = gram_s.shape[0]
    coeffs = (jnp.arange(width, dtype=jnp.int32)[:, None] == chosen[None, :]).astype(jnp.float32)
    factor = jnp.linalg.cholesky(gram_f)
    for step in range(ITERS):
        moved = jnp.dot(cross.T, coeffs, precision=lax.Precision.HIGHEST)
        halfway = lax.linalg.triangular_solve(factor, moved, left_side=True, lower=True)
        solved = lax.linalg.triangular_solve(
            factor, halfway, left_side=True, lower=True, transpose_a=True
        )
        metric = (
            jnp.dot(
                solved.T,
                jnp.dot(gram_s, solved, precision=lax.Precision.HIGHEST),
                precision=lax.Precision.HIGHEST,
            )
            / total_rows
        )
        lower = jnp.linalg.cholesky(metric)
        coeffs = lax.linalg.triangular_solve(
            lower, solved, left_side=False, lower=True, transpose_a=True
        )
    return coeffs


def on_device(basis, image, selection):
    total_rows = basis.shape[1] * lax.axis_size("rows") * lax.axis_size("groups")
    gram_s = jnp.einsum("srk,srl->skl", basis, basis, preferred_element_type=jnp.float32)
    cross = jnp.einsum("srk,srl->skl", basis, image, preferred_element_type=jnp.float32)
    gram_f = jnp.einsum("srk,srl->skl", image, image, preferred_element_type=jnp.float32)
    partial_grams = jnp.stack([gram_s, cross, gram_f], axis=1)
    solver = jax.vmap(lambda grams, chosen: small_solve(grams, chosen, total_rows))
    shares = lax.psum_scatter(partial_grams, "groups", scatter_dimension=0, tiled=True)
    summed = lax.psum(shares, "rows")
    grams = summed
    count = shares.shape[0]
    start = lax.axis_index("groups") * count
    mine = lax.dynamic_slice_in_dim(selection, start, count, 0)
    local_coeffs = solver(grams, mine).astype(jnp.bfloat16)
    narrow = lax.all_gather(local_coeffs, "groups", axis=0, tiled=True)
    first = jnp.einsum("srk,skj->srj", basis, narrow, preferred_element_type=jnp.float32)
    second = jnp.einsum("srk,skj->srj", image, narrow, preferred_element_type=jnp.float32)
    return jnp.concatenate([first, second], axis=2).astype(jnp.bfloat16)


def solution(mesh):
    in_specs = (P(None, ("rows", "groups"), None), P(None, ("rows", "groups"), None), P())
    out_specs = P(None, ("rows", "groups"), None)
    return jax.shard_map(
        on_device, mesh=mesh, in_specs=in_specs, out_specs=out_specs, check_vma=False
    )
```

profile of v0, /device:TPU:0, one launch (start us, length us, event | category | flops | bytes accessed | tf_op | source)
XLA Modules:
  0.0 317.1 jit_solution(13355528183286181943)
XLA Ops:
  6.5 8.5 %convolution_bitcast_fusion.2 = f32[8,1,128,128]{3,2,0,1:T(8,128)S(1)} fusion(bf16[8,4096,128]{2,1,0:T(8,128)(2,1)} %param.10), kind=kOutput, calls=%fused_computation.8 | convolution fusion | flops 1073741824 | bytes 8912896 | tf_op jit(solution)/shard_map/srk,srl->skl/dot_general | solution.py:37
  15.0 5.9 %convolution_bitcast_fusion.1 = f32[8,1,128,128]{3,2,0,1:T(8,128)S(1)} fusion(bf16[8,4096,128]{2,1,0:T(8,128)(2,1)} %param.10, bf16[8,4096,128]{2,1,0:T(8,128)(2,1)S(1)} %copy-done.1), kind=kOutput, calls=%fused_computation.7 | convolution fusion | flops 1073741824 | bytes 17301504 | tf_op jit(solution)/shard_map/srk,srl->skl/dot_general | solution.py:38
  21.0 2.6 convolution_bitcast_fusion
  23.6 0.1 pad_maximum_fusion.1
  23.7 1.6 copy.51
  25.4 0.2 all-reduce.4.cloned.1.call-start
  25.6 0.6 dynamic-slice
  26.9 44.3 %all-reduce.6.cloned.1.call-done = f32[8,3,128,128]{2,3,0,1:T(8,128)} async-done(((f32[8,3,128,128]{2,3,0,1:T(8,128)}), f32[8,3,128,128]{2,3,0,1:T(8,128)}) %all-reduce.6.cloned.1.call-update) | async-done | bytes 1572880
  71.1 1.8 constant_dynamic-slice_fusion
  73.0 73.3 %all-reduce.4.cloned.1.call-done = f32[2,3,128,128]{2,3,0,1:T(8,128)} async-done(((f32[2,3,128,128]{2,3,0,1:T(8,128)}), f32[2,3,128,128]{2,3,0,1:T(8,128)}) %all-reduce.4.cloned.1.call-update) | async-done | bytes 393232 | tf_op jit(solution)/shard_map/psum | solution.py:43
  146.3 0.9 slice_bitcast_fusion.2
  147.2 0.1 copy.52
  147.3 0.9 fusion.3
  148.3 23.5 %custom-call.16 = f32[2,128,128]{2,1,0:T(8,128)S(1)} custom-call(f32[2,128,128]{2,1,0:T(8,128)S(1)} %fusion.3), custom_call_target="Cholesky" | custom-call | tf_op jit(solution)/shard_map/vmap(jit(cholesky))/cholesky | solution.py:13
  171.8 0.1 compare_reduce_fusion.3
  172.0 19.7 %custom-call.34 = f32[2,1,128,128]{2,3,1,0:T(8,128)S(1)} custom-call(f32[2,1,128,128]{3,2,1,0:T(8,128)S(1)} %select_bitcast_fusion), custom_call_target="InvertDiagBlocksLowerTriangular" | custom-call | tf_op jit(solution)/shard_map/vmap()/triangular_solve/custom-call.3 | solution.py:17
  191.7 1.2 fusion.18
  192.8 0.2 fusion.4
  193.1 0.4 fusion.6
  193.5 1.2 fusion.21
  194.6 0.2 convolution_multiply_fusion.2
  195.0 11.7 %custom-call.27 = f32[2,64,64]{2,1,0:T(8,128)S(1)} custom-call(f32[2,64,64]{2,1,0:T(8,128)S(1)} %fusion.27), custom_call_target="Cholesky" | custom-call | tf_op jit(solution)/shard_map/vmap(jit(cholesky))/cholesky | solution.py:28
  206.7 0.1 compare_reduce_fusion.2
  206.9 9.8 %custom-call.28 = f32[2,1,64,64]{2,3,1,0:T(8,128)S(1)} custom-call(f32[2,1,64,64]{3,2,1,0:T(8,128)S(1)} %select_bitcast_fusion.3), custom_call_target="InvertDiagBlocksLowerTriangular" | custom-call | tf_op jit(solution)/shard_map/vmap()/triangular_solve/custom-call.4 | solution.py:29
  216.8 0.3 convolution_bitcast_fusion.5
  217.1 1.3 fusion.17
  218.3 0.2 fusion.8
  218.6 0.4 fusion.10
  219.0 1.2 fusion.20
  220.1 0.2 convolution_multiply_fusion.1
  220.5 11.7 %custom-call.31 = f32[2,64,64]{2,1,0:T(8,128)S(1)} custom-call(f32[2,64,64]{2,1,0:T(8,128)S(1)} %fusion.25), custom_call_target="Cholesky" | custom-call | tf_op jit(solution)/shard_map/vmap(jit(cholesky))/cholesky | solution.py:28
  232.2 0.1 compare_reduce_fusion.1
  232.4 10.0 %custom-call.32 = f32[2,1,64,64]{2,3,1,0:T(8,128)S(1)} custom-call(f32[2,1,64,64]{3,2,1,0:T(8,128)S(1)} %select_bitcast_fusion.2), custom_call_target="InvertDiagBlocksLowerTriangular" | custom-call | tf_op jit(solution)/shard_map/vmap()/triangular_solve/custom-call.4 | solution.py:29
  242.5 0.3 convolution_bitcast_fusion.4
  242.8 1.3 fusion.16
  244.1 0.2 fusion.12
  244.3 0.4 fusion.14
  244.7 1.2 fusion.19
  245.8 0.2 convolution_multiply_fusion
  246.2 11.7 %custom-call.35 = f32[2,64,64]{2,1,0:T(8,128)S(1)} custom-call(f32[2,64,64]{2,1,0:T(8,128)S(1)} %fusion.23), custom_call_target="Cholesky" | custom-call | tf_op jit(solution)/shard_map/vmap(jit(cholesky))/cholesky | solution.py:28
  257.9 0.1 compare_reduce_fusion
  258.1 9.8 %custom-call.36 = f32[2,1,64,64]{2,3,1,0:T(8,128)S(1)} custom-call(f32[2,1,64,64]{3,2,1,0:T(8,128)S(1)} %select_bitcast_fusion.1), custom_call_target="InvertDiagBlocksLowerTriangular" | custom-call | tf_op jit(solution)/shard_map/vmap()/triangular_solve/custom-call.4 | solution.py:29
  268.0 0.3 fusion.2
  268.3 5.4 %all_gather.3 = bf16[8,128,64]{1,2,0:T(8,128)(2,1)S(1)} all-gather(bf16[2,128,64]{1,2,0:T(8,128)(2,1)S(1)} %fusion.2), channel_id=1, replica_groups=mesh['rows'=8,'groups'=4] {'groups'}, dimensions={0}, use_global_device_ids=true | all-gather | bytes 163840 | tf_op jit(solution)/shard_map/all_gather | solution.py:49
  273.7 8.4 %fusion.1 = bf16[8,4096,64]{1,2,0:T(8,128)(2,1)} fusion(bf16[8,128,64]{1,2,0:T(8,128)(2,1)S(1)} %all_gather.3, bf16[8,4096,128]{2,1,0:T(8,128)(2,1)} %param.11), kind=kOutput, calls=%fused_computation.4 | convolution fusion | flops 538968064 | bytes 12713984 | tf_op jit(solution)/shard_map/srk,skj->srj/dot_general | solution.py:51
  282.1 8.4 %fusion = bf16[8,4096,64]{1,2,0:T(8,128)(2,1)} fusion(bf16[8,128,64]{1,2,0:T(8,128)(2,1)S(1)} %all_gather.3, bf16[8,4096,128]{2,1,0:T(8,128)(2,1)} %param.10), kind=kOutput, calls=%fused_computation.3 | convolution fusion | flops 538968064 | bytes 12713984 | tf_op jit(solution)/shard_map/srk,skj->srj/dot_general | solution.py:50
  290.5 7.8 %pad_maximum_fusion = bf16[8,4096,128]{1,2,0:T(8,128)(2,1)} fusion(bf16[8,4096,64]{1,2,0:T(8,128)(2,1)} %fusion.1, bf16[8,4096,64]{1,2,0:T(8,128)(2,1)} %fusion), kind=kLoop, calls=%fused_computation | loop fusion | flops 16777216 | bytes 16777216 | tf_op jit(solution)/shard_map/concatenate | solution.py:52
  298.3 11.9 %copy.79 = bf16[8,4096,128]{2,1,0:T(8,128)(2,1)} copy(bf16[8,4096,128]{1,2,0:T(8,128)(2,1)} %pad_maximum_fusion) | data formatting | bytes 16777216 | tf_op jit(solution)/shard_map/concatenate | solution.py:52
  (28 shorter events, 0.8 us)
Async XLA Ops:
  6.5 66.4 %copy-start = (s32[8,64]{1,0:T(8,128)S(1)}, s32[8,64]{1,0:T(8,128)}, u32[]{:S(2)}) copy-start(s32[8,64]{1,0:T(8,128)} %param.12) | copy-start | bytes 6148
  6.5 64.6 %all-reduce.6.cloned.1.call-start = ((), (), s32[]{:S(2)}) async-start(), calls=%async_computation.1 | async-start | bytes 3145728
  6.5 8.5 %copy-start.1 = (bf16[8,4096,128]{2,1,0:T(8,128)(2,1)S(1)}, bf16[8,4096,128]{2,1,0:T(8,128)(2,1)}, u32[]{:S(2)}) copy-start(bf16[8,4096,128]{2,1,0:T(8,128)(2,1)} %param.11) | copy-start | bytes 25165828
  21.0 4.6 %copy-start.2 = (u32[32]{0:T(128)S(1)}, u32[32]{0:T(128)}, u32[]{:S(2)}) copy-start(u32[32]{0:T(128)} %constant.92) | copy-start | bytes 388
  25.4 120.9 %all-reduce.4.cloned.1.call-start = ((), (), s32[]{:S(2)}) async-start(), calls=%async_computation | async-start | bytes 786432 | tf_op jit(solution)/shard_map/psum | solution.py:43
Sparse Core Ops, SparseCore 0:
  25.5 45.6 all-reduce.5
  74.5 71.7 all-reduce.3
where the time goes:
time: 318 us; the launch traced here: 317 us
  other arithmetic  118 us (37%)
  waiting for transfers between devices  118 us (37%)
  matrix products  44.3 us (14%)
  local copies, waits for them, and re-layouts  17.2 us (5%)
  between operations  14.4 us (5%)
  blocking collectives  5.42 us (2%)
    psum x1, waiting for transfers between devices, on_device(): summed = lax.psum(shares, 'rows')  73.3 us
    unnamed x3, waiting for transfers between devices  44.3 us
    another operation x10, other arithmetic, small_solve(): lower = jnp.linalg.cholesky(metric)  35.6 us
    another operation x7, other arithmetic, small_solve(): lax.linalg.triangular_solve(lower, solved, left_side=False, lower=True, t...  30 us
    another operation x4, other arithmetic, small_solve(): factor = jnp.linalg.cholesky(gram_f)  23.6 us
    another operation x3, other arithmetic, small_solve(): lax.linalg.triangular_solve(factor, halfway, left_side=True, lower=True,...  19.8 us
    concatenate x1, local copies, waits for them, and re-layouts, on_device(): return jnp.concatenate([first, second], axis=2).astype(jnp.bfloat16)  11.9 us
    dot_general x1, matrix products, on_device(): jnp.einsum('srk,srl->skl', basis, basis, preferred_element_type=jnp.float32)  8.47 us
  transfers between devices with their start and end apart: 2, of which 2 were waited for; matrix products, arithmetic and copies ran while one was open for 0% of the time, Pallas kernels for 0%

commit v1 on v0

--- a/solution.py
+++ b/solution.py
@@ -40,7 +40,9 @@
     partial_grams = jnp.stack([gram_s, cross, gram_f], axis=1)
     solver = jax.vmap(lambda grams, chosen: small_solve(grams, chosen, total_rows))
     shares = lax.psum_scatter(partial_grams, "groups", scatter_dimension=0, tiled=True)
-    summed = lax.psum(shares, "rows")
+    summed = shares
+    for hop in (1, 2, 4):
+        summed = summed + lax.ppermute(summed, "rows", [(dev, dev ^ hop) for dev in range(8)])
     grams = summed
     count = shares.shape[0]
     start = lax.axis_index("groups") * count

time: 318 us -> 277 us (0.87)
  waiting for transfers between devices: 118 us -> 78 us
  matrix products: 44.3 us -> 38.9 us
  starting transfers between devices: 0.22 us -> 5.56 us
    psum x1 -> x0, waiting for transfers between devices: 73.3 us -> none  [on_device(): summed = lax.psum(shares, 'rows')]
    ppermute x0 -> x3, waiting for transfers between devices: none -> 33.5 us  [on_device(): lax.ppermute(summed, 'rows', [(dev, dev ^ hop) for dev in range(8)])]
    ppermute x0 -> x3, starting transfers between devices: none -> 5.56 us  [on_device(): lax.ppermute(summed, 'rows', [(dev, dev ^ hop) for dev in range(8)])]
    unnamed x3 -> x2, waiting for transfers between devices: 44.3 us -> 44.5 us
  transfers between devices with their start and end apart: 2 -> 4, of which waited for: 2 -> 4; matrix products, arithmetic and copies ran while one was open for 0% -> 0% of each run, Pallas kernels for 0% -> 0%
where the time goes in v1:
time: 277 us; the launch traced here: 276 us
  other arithmetic  118 us (43%)
  waiting for transfers between devices  78 us (28%)
  matrix products  38.9 us (14%)
  local copies, waits for them, and re-layouts  15.5 us (6%)
  between operations  14.3 us (5%)
  starting transfers between devices  5.56 us (2%)
  blocking collectives  5.42 us (2%)
    unnamed x2, waiting for transfers between devices  44.5 us
    another operation x10, other arithmetic, small_solve(): lower = jnp.linalg.cholesky(metric)  35.6 us
    ppermute x3, waiting for transfers between devices, on_device(): lax.ppermute(summed, 'rows', [(dev, dev ^ hop) for dev in range(8)])  33.5 us
    another operation x7, other arithmetic, small_solve(): lax.linalg.triangular_solve(lower, solved, left_side=False, lower=True, t...  30 us
    another operation x4, other arithmetic, small_solve(): factor = jnp.linalg.cholesky(gram_f)  23.8 us
    another operation x3, other arithmetic, small_solve(): lax.linalg.triangular_solve(factor, halfway, left_side=True, lower=True,...  19.8 us
    concatenate x1, local copies, waits for them, and re-layouts, on_device(): return jnp.concatenate([first, second], axis=2).astype(jnp.bfloat16)  11.9 us
    dot_general x1, matrix products, on_device(): jnp.einsum('srk,srl->skl', basis, basis, preferred_element_type=jnp.float32)  8.47 us
  transfers between devices with their start and end apart: 4, of which 4 were waited for; matrix products, arithmetic and copies ran while one was open for 0% of the time, Pallas kernels for 0%

profile of v1, /device:TPU:0, one launch (start us, length us, event | category | flops | bytes accessed | tf_op | source)
XLA Modules:
  0.0 276.2 jit_solution(5470641913657470030)
XLA Ops:
  6.5 8.5 %convolution_bitcast_fusion.2 = f32[8,1,128,128]{3,2,0,1:T(8,128)S(1)} fusion(bf16[8,4096,128]{2,1,0:T(8,128)(2,1)} %param.10), kind=kOutput, calls=%fused_computation.8 | convolution fusion | flops 1073741824 | bytes 8912896 | tf_op jit(solution)/shard_map/srk,srl->skl/dot_general | solution.py:37
  15.0 5.9 %convolution_bitcast_fusion.1 = f32[8,1,128,128]{3,2,0,1:T(8,128)S(1)} fusion(bf16[8,4096,128]{2,1,0:T(8,128)(2,1)} %param.10, bf16[8,4096,128]{2,1,0:T(8,128)(2,1)S(1)} %copy-done.1), kind=kOutput, calls=%fused_computation.7 | convolution fusion | flops 1073741824 | bytes 17301504 | tf_op jit(solution)/shard_map/srk,srl->skl/dot_general | solution.py:38
  21.0 2.6 convolution_bitcast_fusion
  23.6 0.1 pad_maximum_fusion.1
  23.7 1.6 copy.51
  25.4 0.6 dynamic-slice
  26.6 44.5 %all-reduce.3.cloned.1.call-done = f32[8,3,128,128]{2,3,0,1:T(8,128)} async-done(((f32[8,3,128,128]{2,3,0,1:T(8,128)}), f32[8,3,128,128]{2,3,0,1:T(8,128)}) %all-reduce.3.cloned.1.call-update) | async-done | bytes 1572880
  71.1 1.0 constant_dynamic-slice_fusion
  72.1 1.5 collective-permute-start
  73.6 9.3 %collective-permute-done = f32[2,3,128,128]{2,3,0,1:T(8,128)S(1)} collective-permute-done((f32[2,3,128,128]{2,3,0,1:T(8,128)S(1)}, f32[2,3,128,128]{2,3,0,1:T(8,128)S(1)}, u32[]{:S(2)}, u32[]{:S(2)}) %collective-permute-start) | collective-permute-done | bytes 393248 | tf_op jit(solution)/shard_map/ppermute | solution.py:45
  82.9 1.1 fusion.59
  84.0 1.6 collective-permute-start.1
  85.5 8.4 %collective-permute-done.1 = f32[2,3,128,128]{2,3,0,1:T(8,128)S(1)} collective-permute-done((f32[2,3,128,128]{2,3,0,1:T(8,128)S(1)}, f32[2,3,128,128]{2,3,0,1:T(8,128)S(1)}, u32[]{:S(2)}, u32[]{:S(2)}) %collective-permute-start.1) | collective-permute-done | bytes 393248 | tf_op jit(solution)/shard_map/ppermute | solution.py:45
  94.0 2.5 collective-permute-start.2
  96.5 15.9 %collective-permute-done.2 = f32[2,3,128,128]{2,3,0,1:T(8,128)S(1)} collective-permute-done((f32[2,3,128,128]{2,3,0,1:T(8,128)S(1)}, f32[2,3,128,128]{2,3,0,1:T(8,128)S(1)}, u32[]{:S(2)}, u32[]{:S(2)}) %collective-permute-start.2) | collective-permute-done | bytes 393248 | tf_op jit(solution)/shard_map/ppermute | solution.py:45
  112.5 0.3 fusion.18
  112.9 23.6 %custom-call.16 = f32[2,128,128]{2,1,0:T(8,128)S(1)} custom-call(f32[2,128,128]{2,1,0:T(8,128)S(1)} %fusion.3), custom_call_target="Cholesky" | custom-call | tf_op jit(solution)/shard_map/vmap(jit(cholesky))/cholesky | solution.py:13
  136.8 19.7 %custom-call.34 = f32[2,1,128,128]{2,3,1,0:T(8,128)S(1)} custom-call(f32[2,1,128,128]{3,2,1,0:T(8,128)S(1)} %select_bitcast_fusion), custom_call_target="InvertDiagBlocksLowerTriangular" | custom-call | tf_op jit(solution)/shard_map/vmap()/triangular_solve/custom-call.3 | solution.py:17
  156.4 0.2 fusion.4
  156.7 0.4 fusion.6
  157.1 0.2 fusion.21
  157.3 0.2 convolution_multiply_fusion.2
  157.7 11.7 %custom-call.27 = f32[2,64,64]{2,1,0:T(8,128)S(1)} custom-call(f32[2,64,64]{2,1,0:T(8,128)S(1)} %fusion.27), custom_call_target="Cholesky" | custom-call | tf_op jit(solution)/shard_map/vmap(jit(cholesky))/cholesky | solution.py:28
  169.4 0.1 compare_reduce_fusion.2
  169.6 9.8 %custom-call.28 = f32[2,1,64,64]{2,3,1,0:T(8,128)S(1)} custom-call(f32[2,1,64,64]{3,2,1,0:T(8,128)S(1)} %select_bitcast_fusion.3), custom_call_target="InvertDiagBlocksLowerTriangular" | custom-call | tf_op jit(solution)/shard_map/vmap()/triangular_solve/custom-call.4 | solution.py:29
  179.5 0.3 convolution_bitcast_fusion.5
  179.8 0.4 fusion.17
  180.1 0.2 fusion.8
  180.4 0.4 fusion.10
  180.8 0.2 fusion.20
  181.0 0.2 convolution_multiply_fusion.1
  181.4 11.7 %custom-call.31 = f32[2,64,64]{2,1,0:T(8,128)S(1)} custom-call(f32[2,64,64]{2,1,0:T(8,128)S(1)} %fusion.25), custom_call_target="Cholesky" | custom-call | tf_op jit(solution)/shard_map/vmap(jit(cholesky))/cholesky | solution.py:28
  193.1 0.1 compare_reduce_fusion.1
  193.3 10.0 %custom-call.32 = f32[2,1,64,64]{2,3,1,0:T(8,128)S(1)} custom-call(f32[2,1,64,64]{3,2,1,0:T(8,128)S(1)} %select_bitcast_fusion.2), custom_call_target="InvertDiagBlocksLowerTriangular" | custom-call | tf_op jit(solution)/shard_map/vmap()/triangular_solve/custom-call.4 | solution.py:29
  203.4 0.3 convolution_bitcast_fusion.4
  203.7 0.4 fusion.16
  204.0 0.2 fusion.12
  204.3 0.4 fusion.14
  204.7 0.2 fusion.19
  204.9 0.2 convolution_multiply_fusion
  205.3 11.7 %custom-call.35 = f32[2,64,64]{2,1,0:T(8,128)S(1)} custom-call(f32[2,64,64]{2,1,0:T(8,128)S(1)} %fusion.23), custom_call_target="Cholesky" | custom-call | tf_op jit(solution)/shard_map/vmap(jit(cholesky))/cholesky | solution.py:28
  217.2 9.8 %custom-call.36 = f32[2,1,64,64]{2,3,1,0:T(8,128)S(1)} custom-call(f32[2,1,64,64]{3,2,1,0:T(8,128)S(1)} %select_bitcast_fusion.1), custom_call_target="InvertDiagBlocksLowerTriangular" | custom-call | tf_op jit(solution)/shard_map/vmap()/triangular_solve/custom-call.4 | solution.py:29
  227.1 0.3 fusion.2
  227.4 5.4 %all_gather.3 = bf16[8,128,64]{1,2,0:T(8,128)(2,1)S(1)} all-gather(bf16[2,128,64]{1,2,0:T(8,128)(2,1)S(1)} %fusion.2), channel_id=1, replica_groups=mesh['rows'=8,'groups'=4] {'groups'}, dimensions={0}, use_global_device_ids=true | all-gather | bytes 163840 | tf_op jit(solution)/shard_map/all_gather | solution.py:51
  232.8 8.4 %fusion.1 = bf16[8,4096,64]{1,2,0:T(8,128)(2,1)} fusion(bf16[8,128,64]{1,2,0:T(8,128)(2,1)S(1)} %all_gather.3, bf16[8,4096,128]{2,1,0:T(8,128)(2,1)} %param.11), kind=kOutput, calls=%fused_computation.4 | convolution fusion | flops 538968064 | bytes 12713984 | tf_op jit(solution)/shard_map/srk,skj->srj/dot_general | solution.py:53
  241.2 8.4 %fusion = bf16[8,4096,64]{1,2,0:T(8,128)(2,1)} fusion(bf16[8,128,64]{1,2,0:T(8,128)(2,1)S(1)} %all_gather.3, bf16[8,4096,128]{2,1,0:T(8,128)(2,1)} %param.10), kind=kOutput, calls=%fused_computation.3 | convolution fusion | flops 538968064 | bytes 12713984 | tf_op jit(solution)/shard_map/srk,skj->srj/dot_general | solution.py:52
  249.6 7.8 %pad_maximum_fusion = bf16[8,4096,128]{1,2,0:T(8,128)(2,1)} fusion(bf16[8,4096,64]{1,2,0:T(8,128)(2,1)} %fusion.1, bf16[8,4096,64]{1,2,0:T(8,128)(2,1)} %fusion), kind=kLoop, calls=%fused_computation | loop fusion | flops 16777216 | bytes 16777216 | tf_op jit(solution)/shard_map/concatenate | solution.py:54
  257.4 11.9 %copy.79 = bf16[8,4096,128]{2,1,0:T(8,128)(2,1)} copy(bf16[8,4096,128]{1,2,0:T(8,128)(2,1)} %pad_maximum_fusion) | data formatting | bytes 16777216 | tf_op jit(solution)/shard_map/concatenate | solution.py:54
  (34 shorter events, 1.3 us)
Async XLA Ops:
  6.5 89.9 %copy-start = (s32[8,64]{1,0:T(8,128)S(1)}, s32[8,64]{1,0:T(8,128)}, u32[]{:S(2)}) copy-start(s32[8,64]{1,0:T(8,128)} %param.12) | copy-start | bytes 6148
  6.5 64.5 %all-reduce.3.cloned.1.call-start = ((), (), s32[]{:S(2)}) async-start(), calls=%async_computation | async-start | bytes 3145728
  6.5 8.5 %copy-start.1 = (bf16[8,4096,128]{2,1,0:T(8,128)(2,1)S(1)}, bf16[8,4096,128]{2,1,0:T(8,128)(2,1)}, u32[]{:S(2)}) copy-start(bf16[8,4096,128]{2,1,0:T(8,128)(2,1)} %param.11) | copy-start | bytes 25165828
  21.0 4.4 %copy-start.2 = (u32[32]{0:T(128)S(1)}, u32[32]{0:T(128)}, u32[]{:S(2)}) copy-start(u32[32]{0:T(128)} %constant.92) | copy-start | bytes 388
  72.1 10.8 %collective-permute-start = (f32[2,3,128,128]{2,3,0,1:T(8,128)S(1)}, f32[2,3,128,128]{2,3,0,1:T(8,128)S(1)}, u32[]{:S(2)}, u32[]{:S(2)}) collective-permute-start(f32[2,3,128,128]{2,3,0,1:T(8,128)S(1)} %constant_dynamic-slice_fusion), channel_id=1, source_target_pairs={{0,4},{4,0},{8,12},{12,8},{16,20},{20,16},{24,28},{28,24},{1,5},{5... | collective-permute-start | bytes 1179656 | tf_op jit(solution)/shard_map/ppermute | solution.py:45
  84.0 9.9 %collective-permute-start.1 = (f32[2,3,128,128]{2,3,0,1:T(8,128)S(1)}, f32[2,3,128,128]{2,3,0,1:T(8,128)S(1)}, u32[]{:S(2)}, u32[]{:S(2)}) collective-permute-start(f32[2,3,128,128]{2,3,0,1:T(8,128)S(1)} %fusion.59), channel_id=1, source_target_pairs={{0,8},{4,12},{8,0},{12,4},{16,24},{20,28},{24,16},{28,20},{1,9},{5... | collective-permute-start | bytes 1179656 | tf_op jit(solution)/shard_map/ppermute | solution.py:45
  94.0 18.4 %collective-permute-start.2 = (f32[2,3,128,128]{2,3,0,1:T(8,128)S(1)}, f32[2,3,128,128]{2,3,0,1:T(8,128)S(1)}, u32[]{:S(2)}, u32[]{:S(2)}) collective-permute-start(f32[2,3,128,128]{2,3,0,1:T(8,128)S(1)} %add.34), channel_id=1, source_target_pairs={{0,16},{4,20},{8,24},{12,28},{16,0},{20,4},{24,8},{28,12},{1,17},{... | collective-permute-start | bytes 1179656 | tf_op jit(solution)/shard_map/ppermute | solution.py:45
Sparse Core Ops, SparseCore 0:
  25.5 45.5 all-reduce.2
